TPU v7x, 512 devices: a whole 4x4x16 slice. The times are simulated.
512 devices in a mesh: pts: 128 (over z, x, core), grp: 4 (over y).
Axes of the slice: x: 4, y: 4, z: 16, core: 2. Of those that a mesh axis runs over, the one named last changes fastest.
Arguments:
- vertex_features: bfloat16 [262144, 256], P(('pts', 'grp')), may hold values from -6 to 6
- result_cotangent: bfloat16 [262144, 256], P(('pts', 'grp')), may hold values from -6 to 6
- entry_matrix: bfloat16 [256, 256], replicated, may hold values from -0.375 to 0.375
- exit_matrix: bfloat16 [256, 256], replicated, may hold values from -0.375 to 0.375
- cluster_matrix: bfloat16 [32, 64], replicated, may hold values from -4 to 4
- softmax_sharpness: float32 [8], replicated, may hold values from 0.1 to 2
- cluster_attention_matrices: float32 [3, 32, 32], replicated, may hold values from -2 to 2
- occupied_tally: int32 [512], replicated, may hold values from 170 to 512, as said below
Outputs:
- x_grad: bfloat16 [262144, 256], P(('pts', 'grp'))
- weight_grads: float32 [2, 256, 256], P(None, 'grp')
- slice_grad: float32 [32, 64], replicated
- temp_grad: float32 [8], replicated
- token_grads: float32 [3, 32, 32], replicated
Inputs may be any that keep to these rules, and one draw needn't show every extreme that they name: occupied_tally[i] is the number of valid points of the i-th block of 512 point slots; they come first in the block. Some block is full and some holds 170 in every draw.
All inputs are finite; a program needn't handle non-finite values.
Results may differ from a plain program's by a relative error of at most 0.012.
The roundings to bfloat16 on the way count: a program that leaves them out, or rounds other values in their place, can miss the bound.
Values may be sent and summed in bfloat16 or wider, within the bound.
A program may use at most 64 MiB of HBM per device.

v0:
```python
import jax
import jax.numpy as jnp
from jax import lax
from jax.sharding import Mesh
from jax.sharding import PartitionSpec as P

PTS = ("pts_0", "pts_1", "pts_2")
PTS_GRP = ("pts_0", "pts_1", "pts_2", "grp")


def in_blocks(shard, dim, devices):
    lengths = shard.shape
    parts = shard.reshape(*lengths[:dim], devices, lengths[dim] // devices, *lengths[dim + 1 :])
    return jnp.moveaxis(parts, dim, 0)


def summed_on_arrival(shard, axis, dim):
    devices = lax.axis_size(axis)
    parts = lax.all_to_all(in_blocks(shard, dim, devices), axis, 0, 0, tiled=True)
    return jnp.sum(parts, axis=0)


def sum_by_axis(shard, axes, dim):
    far, near = axes
    parts = in_blocks(shard, dim, lax.axis_size(far))
    nearer = summed_on_arrival(parts, near, dim + 1)
    arrived = lax.all_to_all(nearer, far, split_axis=0, concat_axis=0, tiled=True)
    return arrived.sum(axis=0)


def rows_for(lines, devices):
    spare = -len(lines) % devices
    return jnp.pad(lines, [(0, spare)] + [(0, 0)] * (lines.ndim - 1))


def from_everyone(shard, axis):
    copies = jnp.broadcast_to(shard, (lax.axis_size(axis), *shard.shape))
    return lax.all_to_all(copies, axis, split_axis=0, concat_axis=0, tiled=True)


def joined_along(parts, dim):
    lengths = list(parts.shape[1:])
    lengths[dim] *= parts.shape[0]
    return jnp.moveaxis(parts, 0, dim).reshape(lengths)


def gathered_by_axis(shard, axes, dim):
    far, near = axes
    parts = from_everyone(from_everyone(shard, far), near)
    return joined_along(parts.swapaxes(0, 1).reshape(-1, *shard.shape), dim)


def sum_by_parts(shard, axes):
    own = sum_by_axis(rows_for(shard, lax.axis_size(axes[0]) * lax.axis_size(axes[1])), axes, 0)
    whole = gathered_by_axis(own, axes, 0)
    return whole[: len(shard)].reshape(shard.shape)


def together(arrays, axis):
    ravelled, at, done = (jnp.concatenate([a.reshape(-1) for a in arrays]), 0, [])
    subtotal = sum_by_parts(ravelled, axis)
    for a in arrays:
        done.append(subtotal[at : at + a.size].reshape(a.shape))
        at += a.size
    return tuple(done)


def of_everyone(shard, axis):
    return from_everyone(shard, axis).sum(axis=0)


def by_axis(shard, axes):
    far, near = axes
    return of_everyone(of_everyone(shard, near), far)


def together_2(arrays, axis):
    ravelled, at, done = (jnp.concatenate([a.reshape(-1) for a in arrays]), 0, [])
    subtotal = by_axis(ravelled, axis)
    for a in arrays:
        done.append(subtotal[at : at + a.size].reshape(a.shape))
        at += a.size
    return tuple(done)


def sum_at_owner(shard, axis, dim):
    parts = in_blocks(shard, dim, lax.axis_size(axis))
    arrived = lax.all_to_all(parts, axis, split_axis=0, concat_axis=0, tiled=True)
    return arrived.astype(jnp.float32).sum(axis=0)


def sum_by_parts_2(shard, axes):
    lines = shard.reshape(-1, shard.shape[-1])
    own = sum_by_axis(rows_for(lines, lax.axis_size(axes[0]) * lax.axis_size(axes[1])), axes, 0)
    whole = gathered_by_axis(own, axes, 0)
    return whole[: len(lines)].reshape(shard.shape)


def block_diagonal(parts):
    attention_channels, inner, outer = parts.shape
    unit_matrix = jnp.eye(attention_channels, dtype=parts.dtype)
    spread_out = unit_matrix[:, None, :, None] * parts[:, :, None, :]
    return spread_out.reshape(attention_channels * inner, attention_channels * outer)


def segment_forward_sweep(
    feature_segment,
    result_cotangent_segment,
    validity_flags,
    entry_matrix,
    exit_matrix,
    slice_wide_weights,
    softmax_sharpness,
):
    point_rows = feature_segment.shape[0]
    attention_channels = softmax_sharpness.shape[0]
    xm = jnp.dot(feature_segment, entry_matrix, preferred_element_type=jnp.float32).astype(
        jnp.bfloat16
    )
    unscaled_product = jnp.dot(xm, slice_wide_weights, preferred_element_type=jnp.float32).reshape(
        point_rows, attention_channels, -1
    )
    cluster_scores = unscaled_product / softmax_sharpness[None, :, None]
    cluster_likelihood = jax.nn.softmax(cluster_scores, axis=-1)
    matrix_sequence = (cluster_likelihood * validity_flags[:, None, None]).astype(jnp.bfloat16)
    exit_cotangent = lax.dot_general(
        result_cotangent_segment,
        exit_matrix,
        (((1,), (1,)), ((), ())),
        preferred_element_type=jnp.float32,
    ).astype(jnp.bfloat16)
    return (xm, cluster_scores, cluster_likelihood, matrix_sequence, exit_cotangent)


def slice_middle(
    cluster_dividend, cluster_normalizer, blended_cotangent, cluster_attention_matrices
):
    highest_precision = lax.Precision.HIGHEST
    clip = jnp.maximum(cluster_normalizer, 1.0)
    slice_tokens = cluster_dividend / clip[..., None]
    scale = slice_tokens.shape[-1] ** (-0.5)
    query_rows = jnp.einsum(
        "cui,it->cut", slice_tokens, cluster_attention_matrices[0], precision=highest_precision
    )
    key_rows = jnp.einsum(
        "cui,it->cut", slice_tokens, cluster_attention_matrices[1], precision=highest_precision
    )
    value_rows = jnp.einsum(
        "cui,it->cut", slice_tokens, cluster_attention_matrices[2], precision=highest_precision
    )
    scores = jnp.einsum("hme,hne->hmn", query_rows, key_rows, precision=highest_precision) * scale
    attn = jax.nn.softmax(scores, axis=-1)
    mixed = jnp.einsum("hmn,hne->hme", attn, value_rows, precision=highest_precision)
    value_gradient = jnp.einsum(
        "hmn,hme->hne", attn, blended_cotangent, precision=highest_precision
    )
    g_attn = jnp.einsum("hme,hne->hmn", blended_cotangent, value_rows, precision=highest_precision)
    g_scores = attn * (g_attn - jnp.sum(g_attn * attn, axis=-1, keepdims=True)) * scale
    query_gradient = jnp.einsum("hmn,hne->hme", g_scores, key_rows, precision=highest_precision)
    key_gradient = jnp.einsum("hmn,hme->hne", g_scores, query_rows, precision=highest_precision)
    query_map_gradient = jnp.einsum(
        "sul,suv->lv", slice_tokens, query_gradient, precision=highest_precision
    )
    key_map_gradient = jnp.einsum(
        "sul,suv->lv", slice_tokens, key_gradient, precision=highest_precision
    )
    value_map_gradient = jnp.einsum(
        "sul,suv->lv", slice_tokens, value_gradient, precision=highest_precision
    )
    token_gradient = jnp.einsum(
        "cqr,jr->cqj", query_gradient, cluster_attention_matrices[0], precision=highest_precision
    )
    token_gradient = token_gradient + jnp.einsum(
        "cqr,jr->cqj", key_gradient, cluster_attention_matrices[1], precision=highest_precision
    )
    token_gradient = token_gradient + jnp.einsum(
        "cqr,jr->cqj", value_gradient, cluster_attention_matrices[2], precision=highest_precision
    )
    g_num = token_gradient / clip[..., None]
    normalizer_cotangent = jnp.where(
        cluster_normalizer > 1.0, -jnp.sum(token_gradient * slice_tokens, axis=-1) / clip, 0.0
    )
    return (
        mixed,
        g_num,
        normalizer_cotangent,
        jnp.stack([query_map_gradient, key_map_gradient, value_map_gradient]),
    )


def local(
    vertex_features,
    result_cotangent,
    entry_matrix,
    exit_matrix,
    cluster_matrix,
    softmax_sharpness,
    cluster_attention_matrices,
    occupied_tally,
):
    point_rows = vertex_features.shape[0]
    width = vertex_features.shape[1]
    attention_channels = softmax_sharpness.shape[0]
    head = width // attention_channels
    slices = cluster_matrix.shape[1]
    block = min(512, point_rows)
    groups = lax.axis_size("grp")
    device = lax.axis_index(PTS) * groups + lax.axis_index("grp")
    owner_pick = jnp.arange(occupied_tally.shape[0], dtype=jnp.int32) == device
    valid = jnp.sum(jnp.where(owner_pick, occupied_tally, 0))
    x_rows, y_rows = (vertex_features, result_cotangent)
    trips = point_rows // block
    slice_wide_weights = block_diagonal(
        jnp.broadcast_to(cluster_matrix, (attention_channels, head, slices))
    )
    slice_back = block_diagonal(
        jnp.broadcast_to(cluster_matrix.T, (attention_channels, slices, head))
    )

    def take(index):
        begin = index * block
        validity_flags = (begin + jnp.arange(block, dtype=jnp.int32) < valid).astype(jnp.float32)
        return (begin, x_rows, y_rows, validity_flags)

    def first(index, loop_state):
        begin, feature_segment, result_cotangent_segment, validity_flags = take(index)
        xm, cluster_scores, cluster_likelihood, matrix_sequence, exit_cotangent = (
            segment_forward_sweep(
                feature_segment,
                result_cotangent_segment,
                validity_flags,
                entry_matrix,
                exit_matrix,
                slice_wide_weights,
                softmax_sharpness,
            )
        )
        cluster_dividend = jnp.einsum(
            "fzs,fzb->zsb",
            matrix_sequence,
            xm.reshape(block, attention_channels, head),
            preferred_element_type=jnp.float32,
        )
        cluster_normalizer = jnp.sum(matrix_sequence, axis=0, dtype=jnp.float32)
        blended_cotangent = jnp.einsum(
            "fzs,fzb->zsb",
            matrix_sequence,
            exit_cotangent.reshape(block, attention_channels, head),
            preferred_element_type=jnp.float32,
        )
        return (
            loop_state[0] + cluster_dividend,
            loop_state[1] + cluster_normalizer,
            loop_state[2] + blended_cotangent,
        )

    start = (
        jnp.zeros((attention_channels, slices, head), jnp.float32),
        jnp.zeros((attention_channels, slices), jnp.float32),
        jnp.zeros((attention_channels, slices, head), jnp.float32),
    )
    partial_sums = lax.fori_loop(0, trips, first, start)
    cluster_dividend, cluster_normalizer, blended_cotangent = together(
        (partial_sums[0], partial_sums[1], partial_sums[2]), (("pts_0", "pts_1"), ("pts_2", "grp"))
    )
    mixed, g_num, normalizer_cotangent, token_grads = slice_middle(
        cluster_dividend, cluster_normalizer, blended_cotangent, cluster_attention_matrices
    )
    blended_bottom_share = mixed.astype(jnp.bfloat16)
    dividend_bottom_share = g_num.astype(jnp.bfloat16)
    merge_table = block_diagonal(blended_bottom_share)
    score_mixed = block_diagonal(jnp.swapaxes(blended_bottom_share, 1, 2))
    score_num = block_diagonal(jnp.swapaxes(dividend_bottom_share, 1, 2))
    back_num = block_diagonal(dividend_bottom_share)

    def second(index, loop_state):
        features_finished, cotangent_sequence, cluster_matrix_cotangent, sharpness_cotangent = (
            loop_state
        )
        begin, feature_segment, result_cotangent_segment, validity_flags = take(index)
        xm, cluster_scores, cluster_likelihood, matrix_sequence, exit_cotangent = (
            segment_forward_sweep(
                feature_segment,
                result_cotangent_segment,
                validity_flags,
                entry_matrix,
                exit_matrix,
                slice_wide_weights,
                softmax_sharpness,
            )
        )
        flat_weights = matrix_sequence.reshape(block, -1)
        merged_heads = jnp.dot(
            flat_weights, merge_table, preferred_element_type=jnp.float32
        ).astype(jnp.bfloat16)
        exit_matrix_cotangent = lax.dot_general(
            merged_heads,
            result_cotangent_segment,
            (((0,), (0,)), ((), ())),
            preferred_element_type=jnp.float32,
        )
        assign_weight_gradient = jnp.dot(
            exit_cotangent, score_mixed, preferred_element_type=jnp.float32
        )
        assign_weight_gradient = assign_weight_gradient + jnp.dot(
            xm, score_num, preferred_element_type=jnp.float32
        )
        assign_weight_gradient = (
            assign_weight_gradient.reshape(block, attention_channels, slices)
            + normalizer_cotangent[None]
        ) * validity_flags[:, None, None]
        score_cotangent = cluster_likelihood * (
            assign_weight_gradient
            - jnp.sum(assign_weight_gradient * cluster_likelihood, axis=-1, keepdims=True)
        )
        unscaled_cotangent = (score_cotangent / softmax_sharpness[None, :, None]).astype(
            jnp.bfloat16
        )
        g_xm = jnp.dot(flat_weights, back_num, preferred_element_type=jnp.float32)
        g_xm = g_xm + jnp.dot(
            unscaled_cotangent.reshape(block, -1), slice_back, preferred_element_type=jnp.float32
        )
        g_xm = g_xm.astype(jnp.bfloat16)
        slice_part = lax.dot_general(
            xm.reshape(block, attention_channels, head),
            unscaled_cotangent,
            (((0, 1), (0, 1)), ((), ())),
            preferred_element_type=jnp.float32,
        )
        sharpness_share = (
            -jnp.sum(score_cotangent * cluster_scores, axis=(0, 2)) / softmax_sharpness
        )
        feature_cotangent = lax.dot_general(
            g_xm, entry_matrix, (((1,), (1,)), ((), ())), preferred_element_type=jnp.float32
        ).astype(jnp.bfloat16)
        entry_matrix_cotangent = lax.dot_general(
            feature_segment, g_xm, (((0,), (0,)), ((), ())), preferred_element_type=jnp.float32
        )
        features_finished = feature_cotangent
        cotangent_sequence = cotangent_sequence + jnp.stack(
            [entry_matrix_cotangent, exit_matrix_cotangent]
        )
        return (
            features_finished,
            cotangent_sequence,
            cluster_matrix_cotangent + slice_part,
            sharpness_cotangent + sharpness_share,
        )

    start2 = (
        jnp.zeros((point_rows, width), jnp.bfloat16),
        jnp.zeros((2, width, width), jnp.float32),
        jnp.zeros((head, slices), jnp.float32),
        jnp.zeros((attention_channels,), jnp.float32),
    )
    features_finished, local_grads, slice_local, temp_local = lax.fori_loop(
        0, trips, second, start2
    )
    slice_grad, temp_grad = together_2(
        (slice_local, temp_local), (("pts_0", "pts_1"), ("pts_2", "grp"))
    )
    owned = sum_at_owner(local_grads.astype(jnp.bfloat16), "grp", 1)
    weight_grads = sum_by_parts_2(owned, (("pts_0", "pts_1"), "pts_2"))
    return (features_finished, weight_grads, slice_grad, temp_grad, token_grads)


def solution(mesh):
    finer = Mesh(
        mesh.devices.reshape(16, 4, 2, mesh.shape["grp"]), ("pts_0", "pts_1", "pts_2", "grp")
    )
    placed = (P(PTS_GRP, None), P(PTS_GRP, None), P(), P(), P(), P(), P(), P())
    return jax.shard_map(
        local,
        mesh=finer,
        in_specs=placed,
        out_specs=(P(PTS_GRP, None), P(None, "grp", None), P(), P(), P()),
        check_vma=False,
    )
```

profile of v0, /device:TPU:1, one launch (start us, length us, event | category | flops | bytes accessed | tf_op | source)
XLA Modules:
  0.0 217.3 jit_solution(1244612192367696865)
XLA Ops:
  8.6 15.8 %all_to_all.68 = f32[8,64,65]{2,1,0:T(8,128)S(1)} all-to-all(f32[8,64,65]{2,1,0:T(8,128)S(1)} %copy.173), channel_id=1, replica_groups=mesh['pts_0'=16,'pts_1'=4,'pts_2'=2,'grp'=4] {'pts_2','grp'}, dimensions={0} | all-to-all | bytes 266240 | tf_op jit(solution)/shard_map/all_to_all | solution.py:19
  24.4 28.1 %all_to_all.69 = f32[64,1,65]{2,1,0:T(1,128)S(1)} all-to-all(f32[64,1,65]{2,1,0:T(1,128)S(1)} %bitcast.162), channel_id=1, replica_groups=mesh['pts_0'=16,'pts_1'=4,'pts_2'=2,'grp'=4] {'pts_0','pts_1'}, dimensions={0} | all-to-all | bytes 33280 | tf_op jit(solution)/shard_map/all_to_all | solution.py:27
  52.6 17.4 %all_to_all.70 = f32[64,1,65]{2,1,0:T(1,128)S(1)} all-to-all(f32[64,1,65]{2,1,0:T(1,128)S(1)} %broadcast_in_dim.35), channel_id=1, replica_groups=mesh['pts_0'=16,'pts_1'=4,'pts_2'=2,'grp'=4] {'pts_0','pts_1'}, dimensions={0} | all-to-all | bytes 33280 | tf_op jit(solution)/shard_map/all_to_all | solution.py:38
  70.7 6.2 %all-to-all-start.3 = ((f32[8,64,65]{2,1,0:T(8,128)}), f32[8,64,65]{2,1,0:T(8,128)S(1)}, u32[]{:S(2)}, u32[]{:S(2)}) async-start(f32[8,64,65]{2,1,0:T(8,128)} %broadcast_in_dim.36), calls=%async_computation.3 | async-start | bytes 524288 | tf_op jit(solution)/shard_map/all_to_all | solution.py:38
  76.9 1.3 convolution_divide_fusion
  78.3 5.2 %all-to-all-done.3 = f32[8,64,65]{2,1,0:T(8,128)S(1)} async-done(((f32[8,64,65]{2,1,0:T(8,128)}), f32[8,64,65]{2,1,0:T(8,128)S(1)}, u32[]{:S(2)}, u32[]{:S(2)}) %all-to-all-start.3) | async-done | bytes 133152 | tf_op jit(solution)/shard_map/all_to_all | solution.py:38
  95.2 1.3 divide_select_fusion
  96.5 1.8 broadcast_multiply_fusion
  98.4 2.1 mul.192
  100.5 1.0 mul.204
  107.4 3.4 %all-to-all-start.4 = ((bf16[4,2,64,256]{3,2,1,0:T(8,128)(2,1)}), bf16[4,2,64,256]{3,2,1,0:T(8,128)(2,1)S(1)}, u32[]{:S(2)}, u32[]{:S(2)}) async-start(bf16[4,2,64,256]{3,2,1,0:T(8,128)(2,1)} %maximum_bitcast_fusion), calls=%async_computation.4 | async-start | bytes 524288 | tf_op jit(solution)/shard_map/all_to_all | solution.py:88
  111.2 5.8 %all-to-all-done.4 = bf16[4,2,64,256]{3,2,1,0:T(8,128)(2,1)S(1)} async-done(((bf16[4,2,64,256]{3,2,1,0:T(8,128)(2,1)}), bf16[4,2,64,256]{3,2,1,0:T(8,128)(2,1)S(1)}, u32[]{:S(2)}, u32[]{:S(2)}) %all-to-all-start.4) | async-done | bytes 262176 | tf_op jit(solution)/shard_map/all_to_all | solution.py:88
  117.1 5.0 %all_to_all.71 = f32[2,64,1,256]{3,1,2,0:T(8,128)S(1)} all-to-all(f32[2,64,1,256]{3,1,2,0:T(8,128)S(1)} %copy.197), channel_id=1, replica_groups=mesh['pts_0'=16,'pts_1'=4,'pts_2'=2,'grp'=4] {'pts_2'}, dimensions={0} | all-to-all | bytes 262144 | tf_op jit(solution)/shard_map/all_to_all | solution.py:19
  122.7 4.6 %all-to-all-start.6 = ((f32[64,1,256]{2,1,0:T(1,128)}), f32[64,1,256]{2,1,0:T(1,128)S(1)}, u32[]{:S(2)}, u32[]{:S(2)}) async-start(f32[64,1,256]{2,1,0:T(1,128)} %reduce_sum.157), calls=%async_computation.6 | async-start | bytes 131072 | tf_op jit(solution)/shard_map/all_to_all | solution.py:27
  127.4 14.1 %all-to-all-done.6 = f32[64,1,256]{2,1,0:T(1,128)S(1)} async-done(((f32[64,1,256]{2,1,0:T(1,128)}), f32[64,1,256]{2,1,0:T(1,128)S(1)}, u32[]{:S(2)}, u32[]{:S(2)}) %all-to-all-start.6) | async-done | bytes 65568 | tf_op jit(solution)/shard_map/all_to_all | solution.py:27
  142.2 5.4 %all-to-all-start.9 = ((f32[8,1,2056]{2,1,0:T(1,128)}), f32[8,1,2056]{2,1,0:T(1,128)S(1)}, u32[]{:S(2)}, u32[]{:S(2)}) async-start(f32[8,1,2056]{2,1,0:T(1,128)} %broadcast_in_dim.40), calls=%async_computation.9 | async-start | bytes 139264 | tf_op jit(solution)/shard_map/all_to_all | solution.py:38
  147.7 4.9 %all-to-all-done.9 = f32[8,1,2056]{2,1,0:T(1,128)S(1)} async-done(((f32[8,1,2056]{2,1,0:T(1,128)}), f32[8,1,2056]{2,1,0:T(1,128)S(1)}, u32[]{:S(2)}, u32[]{:S(2)}) %all-to-all-start.9) | async-done | bytes 65824 | tf_op jit(solution)/shard_map/all_to_all | solution.py:38
  153.2 4.6 %all-to-all-start.7 = ((f32[64,1,256]{2,1,0:T(1,128)}), f32[64,1,256]{2,1,0:T(1,128)S(1)}, u32[]{:S(2)}, u32[]{:S(2)}) async-start(f32[64,1,256]{2,1,0:T(1,128)} %broadcast_in_dim.38), calls=%async_computation.7 | async-start | bytes 131072 | tf_op jit(solution)/shard_map/all_to_all | solution.py:38
  157.9 14.1 %all-to-all-done.7 = f32[64,1,256]{2,1,0:T(1,128)S(1)} async-done(((f32[64,1,256]{2,1,0:T(1,128)}), f32[64,1,256]{2,1,0:T(1,128)S(1)}, u32[]{:S(2)}, u32[]{:S(2)}) %all-to-all-start.7) | async-done | bytes 65568 | tf_op jit(solution)/shard_map/all_to_all | solution.py:38
  172.0 5.4 %all_to_all.72 = f32[2,64,1,256]{3,1,2,0:T(8,128)S(1)} all-to-all(f32[2,64,1,256]{3,1,2,0:T(8,128)S(1)} %broadcast_in_dim.39), channel_id=1, replica_groups=mesh['pts_0'=16,'pts_1'=4,'pts_2'=2,'grp'=4] {'pts_2'}, dimensions={0} | all-to-all | bytes 262144 | tf_op jit(solution)/shard_map/all_to_all | solution.py:38
  177.4 1.1 broadcast_in_dim.49
  178.4 4.8 %all-to-all-start.10 = ((f32[64,1,2056]{2,1,0:T(1,128)}), f32[64,1,2056]{2,1,0:T(1,128)S(1)}, u32[]{:S(2)}, u32[]{:S(2)}) async-start(f32[64,1,2056]{2,1,0:T(1,128)} %broadcast_in_dim.49), calls=%async_computation.10 | async-start | bytes 1114112 | tf_op jit(solution)/shard_map/all_to_all | solution.py:38
  185.9 1.0 convolution_convert_fusion.1
  187.7 28.0 %all-to-all-done.10 = f32[64,1,2056]{2,1,0:T(1,128)S(1)} async-done(((f32[64,1,2056]{2,1,0:T(1,128)}), f32[64,1,2056]{2,1,0:T(1,128)S(1)}, u32[]{:S(2)}, u32[]{:S(2)}) %all-to-all-start.10) | async-done | bytes 526368 | tf_op jit(solution)/shard_map/all_to_all | solution.py:38
  (144 shorter events, 33.7 us)
Async XLA Ops:
  0.6 2.7 %copy-start = (bf16[512,256]{1,0:T(8,128)(2,1)S(1)}, bf16[512,256]{1,0:T(8,128)(2,1)}, u32[]{:S(2)}) copy-start(bf16[512,256]{1,0:T(8,128)(2,1)} %param.8) | copy-start | bytes 786436
  0.7 2.1 copy-start.17
  2.7 2.9 %copy-start.20 = (f32[512]{0:T(512)}, f32[512]{0:T(512)S(1)}, u32[]{:S(2)}) copy-start(f32[512]{0:T(512)S(1)} %fusion.36) | copy-start | bytes 6148
  3.2 0.9 copy-start.5
  5.5 1.0 copy-start.2
  6.5 1.0 copy-start.7
  70.7 12.8 %all-to-all-start.3 = ((f32[8,64,65]{2,1,0:T(8,128)}), f32[8,64,65]{2,1,0:T(8,128)S(1)}, u32[]{:S(2)}, u32[]{:S(2)}) async-start(f32[8,64,65]{2,1,0:T(8,128)} %broadcast_in_dim.36), calls=%async_computation.3 | async-start | bytes 524288 | tf_op jit(solution)/shard_map/all_to_all | solution.py:38
  90.0 1.9 copy-start.15
  90.6 1.5 copy-start.11
  91.2 1.2 copy-start.26
  101.5 0.9 copy-start.1
  101.5 1.3 copy-start.28
  101.9 1.3 copy-start.3
  103.5 0.9 copy-start.4
  105.1 1.0 copy-start.8
  107.4 9.5 %all-to-all-start.4 = ((bf16[4,2,64,256]{3,2,1,0:T(8,128)(2,1)}), bf16[4,2,64,256]{3,2,1,0:T(8,128)(2,1)S(1)}, u32[]{:S(2)}, u32[]{:S(2)}) async-start(bf16[4,2,64,256]{3,2,1,0:T(8,128)(2,1)} %maximum_bitcast_fusion), calls=%async_computation.4 | async-start | bytes 524288 | tf_op jit(solution)/shard_map/all_to_all | solution.py:88
  122.7 18.8 %all-to-all-start.6 = ((f32[64,1,256]{2,1,0:T(1,128)}), f32[64,1,256]{2,1,0:T(1,128)S(1)}, u32[]{:S(2)}, u32[]{:S(2)}) async-start(f32[64,1,256]{2,1,0:T(1,128)} %reduce_sum.157), calls=%async_computation.6 | async-start | bytes 131072 | tf_op jit(solution)/shard_map/all_to_all | solution.py:27
  142.2 10.3 %all-to-all-start.9 = ((f32[8,1,2056]{2,1,0:T(1,128)}), f32[8,1,2056]{2,1,0:T(1,128)S(1)}, u32[]{:S(2)}, u32[]{:S(2)}) async-start(f32[8,1,2056]{2,1,0:T(1,128)} %broadcast_in_dim.40), calls=%async_computation.9 | async-start | bytes 139264 | tf_op jit(solution)/shard_map/all_to_all | solution.py:38
  153.2 18.8 %all-to-all-start.7 = ((f32[64,1,256]{2,1,0:T(1,128)}), f32[64,1,256]{2,1,0:T(1,128)S(1)}, u32[]{:S(2)}, u32[]{:S(2)}) async-start(f32[64,1,256]{2,1,0:T(1,128)} %broadcast_in_dim.38), calls=%async_computation.7 | async-start | bytes 131072 | tf_op jit(solution)/shard_map/all_to_all | solution.py:38
  178.4 4.8 %copy-start.14 = (f32[8,64,32]{1,2,0:T(8,128)S(1)}, f32[8,64,32]{1,2,0:T(8,128)}, u32[]{:S(2)}) copy-start(f32[8,64,32]{1,2,0:T(8,128)} %copy-done.13) | copy-start | bytes 196612
  178.4 4.8 %copy-start.16 = (f32[8,64,32]{1,2,0:T(8,128)S(1)}, f32[8,64,32]{1,2,0:T(8,128)}, u32[]{:S(2)}) copy-start(f32[8,64,32]{1,2,0:T(8,128)} %copy-done.15) | copy-start | bytes 196612
  178.4 37.3 %all-to-all-start.10 = ((f32[64,1,2056]{2,1,0:T(1,128)}), f32[64,1,2056]{2,1,0:T(1,128)S(1)}, u32[]{:S(2)}, u32[]{:S(2)}) async-start(f32[64,1,2056]{2,1,0:T(1,128)} %broadcast_in_dim.49), calls=%async_computation.10 | async-start | bytes 1114112 | tf_op jit(solution)/shard_map/all_to_all | solution.py:38
  183.2 0.9 copy-start.12
  184.1 0.9 copy-start.27
  (11 other events, 8.4 us)
where the time goes:
time: 220 us; the launch traced here: 217 us
  waiting for transfers between devices  72 us (33%)
  blocking collectives  71.6 us (33%)
  starting transfers between devices  29 us (13%)
  local copies, waits for them, and re-layouts  22.1 us (10%)
  matrix products  13.5 us (6%)
  other arithmetic  7.73 us (4%)
    all_to_all x4, waiting for transfers between devices, from_everyone(): return lax.all_to_all(copies, axis, split_axis=0, concat_axis=0, tiled=True)  52.1 us
    all_to_all x1, blocking collectives, sum_by_axis(): lax.all_to_all(nearer, far, split_axis=0, concat_axis=0, tiled=True)  28.1 us
    all_to_all x2, blocking collectives, from_everyone(): return lax.all_to_all(copies, axis, split_axis=0, concat_axis=0, tiled=True)  22.8 us
    all_to_all x4, starting transfers between devices, from_everyone(): return lax.all_to_all(copies, axis, split_axis=0, concat_axis=0, tiled=True)  21 us
    all_to_all x2, blocking collectives, summed_on_arrival(): lax.all_to_all(in_blocks(shard, dim, devices), axis, 0, 0, tiled=True)  20.8 us
    all_to_all x1, waiting for transfers between devices, sum_by_axis(): lax.all_to_all(nearer, far, split_axis=0, concat_axis=0, tiled=True)  14.1 us
    unnamed x59, local copies, waits for them, and re-layouts  8.1 us
    all_to_all x1, waiting for transfers between devices, sum_at_owner(): lax.all_to_all(parts, axis, split_axis=0, concat_axis=0, tiled=True)  5.77 us
  transfers between devices with their start and end apart: 6, of which 6 were waited for; matrix products, arithmetic and copies ran while one was open for 2% of the time, Pallas kernels for 0%

commit v1 on v0

v1 whole, which is shorter than its diff:
```python
import functools

import jax
import jax.numpy as jnp
from jax import lax
from jax.experimental import pallas as pl
from jax.experimental.pallas import tpu as pltpu
from jax.sharding import Mesh
from jax.sharding import PartitionSpec as P

SIDE, GRP = 8, 4
PLANE = SIDE * GRP
HEADS, SLICES, HEAD, WIDTH = 8, 64, 32, 256
PAIRS = HEADS // 2
F32, BF16 = jnp.float32, jnp.bfloat16
EXACT = lax.Precision.HIGHEST


def dot(a, b, ca=1, cb=0, precision=None):
    return lax.dot_general(
        a, b, (((ca,), (cb,)), ((), ())), preferred_element_type=F32, precision=precision
    )


def kernel(
    depth,
    x_ref,
    y_ref,
    w_ref,
    e_ref,
    c_ref,
    t_ref,
    a_ref,
    tally_ref,
    dx_ref,
    dw_ref,
    ds_ref,
    dt_ref,
    da_ref,
    xmt,
    got,
    prob,
    logit,
    wgt,
    mrg,
    gxm,
    xt,
    tok_out,
    den_out,
    tok_in,
    den_in,
    tok_part,
    den_part,
    tok_z,
    den_z,
    tok_sum,
    den_sum,
    tok_all,
    den_all,
    g_out,
    g_in,
    s_out,
    s_in,
    g_part,
    s_part,
    g_z,
    s_z,
    g_sum,
    s_sum,
    g_all,
    s_all,
    send_sem,
    recv_sem,
):
    z, s, y = lax.axis_index("z"), lax.axis_index("s"), lax.axis_index("y")
    me = s * GRP + y
    points = x_ref.shape[0]

    def plane_peer(r):
        other = lax.rem(me + r, PLANE)
        return other, (z, other // GRP, lax.rem(other, GRP))

    def depth_peer(r):
        return (lax.rem(z + r, depth), s, y)

    def side_peer(r):
        return (z, lax.rem(s + r, SIDE), y)

    barrier = pltpu.get_barrier_semaphore()

    def greet_plane(r, carry):
        pl.semaphore_signal(
            barrier, inc=1, device_id=plane_peer(r)[1], device_id_type=pl.DeviceIdType.MESH
        )
        return carry

    def greet_depth(r, carry):
        pl.semaphore_signal(
            barrier, inc=1, device_id=depth_peer(r), device_id_type=pl.DeviceIdType.MESH
        )
        return carry

    lax.fori_loop(1, PLANE, greet_plane, 0)
    lax.fori_loop(1, depth, greet_depth, 0)

    def push(src, dst, lane, peer):
        pltpu.make_async_remote_copy(
            src_ref=src,
            dst_ref=dst,
            send_sem=send_sem.at[lane],
            recv_sem=recv_sem.at[lane],
            device_id=peer,
            device_id_type=pl.DeviceIdType.MESH,
        ).start()

    def landed(ref, lane):
        pltpu.make_async_copy(ref, ref, recv_sem.at[lane]).wait()

    def left(ref, lane):
        pltpu.make_async_copy(ref, ref, send_sem.at[lane]).wait()

    live = (
        lax.broadcasted_iota(jnp.int32, (1, points), 1) < tally_ref[z * PLANE + me]
    ).astype(F32)
    xm_all = dot(w_ref[...], x_ref[...], 0, 1).astype(BF16)
    xmt[...] = xm_all
    go_all = dot(e_ref[...], y_ref[...], 1, 1).astype(BF16)
    got[...] = go_all
    cluster = c_ref[...]
    cluster_t = cluster.astype(F32).T.astype(BF16)
    half = lax.broadcasted_iota(jnp.int32, (1, 2 * SLICES), 1) < SLICES
    ones = jnp.ones((2 * 8, points), BF16)
    rates = []
    for pair in range(PAIRS):
        for h in (2 * pair, 2 * pair + 1):
            rate = 1.0 / jnp.full((1, points), t_ref[h], F32)
            rates.append(rate)
            xm = xm_all[h * HEAD : (h + 1) * HEAD]
            raw = dot(cluster_t, xm) * rate
            e = jnp.exp(raw - jnp.max(raw, axis=0, keepdims=True))
            p = e * (1.0 / jnp.sum(e, axis=0, keepdims=True))
            rows = pl.ds(h * SLICES, SLICES)
            logit[rows, :] = raw
            prob[rows, :] = p
            wgt[rows, :] = (p * live).astype(BF16)
        w2 = wgt[pl.ds(pair * 2 * SLICES, 2 * SLICES), :]
        parts = []
        for h in (2 * pair, 2 * pair + 1):
            rows = slice(h * HEAD, (h + 1) * HEAD)
            parts.append(dot(jnp.concatenate([xm_all[rows], go_all[rows], ones]), w2, 1, 1))
        both = jnp.where(half, parts[0], parts[1])
        tok_out[pl.ds(pair * 8, 8)] = both[: 2 * HEAD].reshape(8, 8, 2 * SLICES)
        den_out[pl.ds(pair * 8, 8)] = both[2 * HEAD : 2 * HEAD + 8].reshape(8, 1, 2 * SLICES)

    pl.semaphore_wait(barrier, PLANE - 1 + depth - 1)

    def scatter_tokens(r, carry):
        other, peer = plane_peer(r)
        push(tok_out.at[other], tok_in.at[r], 0, peer)
        push(den_out.at[other], den_in.at[r], 1, peer)
        return carry

    lax.fori_loop(1, PLANE, scatter_tokens, 0)
    tok_in[0] = tok_out[me]
    den_in[0] = den_out[me]
    xt[...] = x_ref[...].T
    landed(tok_in.at[pl.ds(1, PLANE - 1)], 0)
    landed(den_in.at[pl.ds(1, PLANE - 1)], 1)
    tok_part[...] = jnp.sum(tok_in[...], axis=0)
    den_part[...] = jnp.sum(den_in[...], axis=0)

    def swap_tokens(r, carry):
        push(tok_part, tok_z.at[z], 2, depth_peer(r))
        push(den_part, den_z.at[z], 3, depth_peer(r))
        return carry

    lax.fori_loop(1, depth, swap_tokens, 0)
    tok_z[z] = tok_part[...]
    den_z[z] = den_part[...]
    landed(tok_z.at[pl.ds(0, depth - 1)], 2)
    landed(den_z.at[pl.ds(0, depth - 1)], 3)
    tok_sum[...] = jnp.sum(tok_z[...], axis=0)
    den_sum[...] = jnp.sum(den_z[...], axis=0)

    def spread_tokens(r, carry):
        peer = plane_peer(r)[1]
        push(tok_sum, tok_all.at[me], 4, peer)
        push(den_sum, den_all.at[me], 5, peer)
        return carry

    lax.fori_loop(1, PLANE, spread_tokens, 0)
    tok_all[me] = tok_sum[...]
    den_all[me] = den_sum[...]
    landed(tok_all.at[pl.ds(1, PLANE - 1)], 4)
    landed(den_all.at[pl.ds(1, PLANE - 1)], 5)

    tok4 = tok_all[...].reshape(PAIRS, 2 * HEAD, 2 * SLICES)
    num = jnp.concatenate([tok4[i, :HEAD] for i in range(PAIRS)], axis=1)
    g_mix = jnp.concatenate([tok4[i, HEAD:] for i in range(PAIRS)], axis=1)
    den = jnp.concatenate([den_all[8 * i] for i in range(PAIRS)], axis=1)
    clip = jnp.maximum(den, 1.0)
    inverse = 1.0 / clip
    tokens = num * inverse
    maps = [a_ref[i] for i in range(3)]
    maps_t = jnp.concatenate([m.T for m in maps])
    qkv = dot(maps_t, tokens, precision=EXACT)
    q_t, k_t, v_t = qkv[:HEAD], qkv[HEAD : 2 * HEAD], qkv[2 * HEAD :]
    k_n, v_n = k_t.T, v_t.T
    scale = HEAD ** (-0.5)

    def on_diagonal(block):
        return jnp.concatenate([jnp.where(half, block, 0.0), jnp.where(half, 0.0, block)])

    mixed, grads = [], []
    for pair in range(PAIRS):
        cols = slice(pair * 2 * SLICES, (pair + 1) * 2 * SLICES)
        low = slice(pair * 2 * SLICES, pair * 2 * SLICES + SLICES)
        high = slice(pair * 2 * SLICES + SLICES, (pair + 1) * 2 * SLICES)
        q2, k2, v2, g2 = q_t[:, cols], k_t[:, cols], v_t[:, cols], g_mix[:, cols]
        scores = scale * jnp.where(
            half, dot(k_n[low], q2, precision=EXACT), dot(k_n[high], q2, precision=EXACT)
        )
        e = jnp.exp(scores - jnp.max(scores, axis=0, keepdims=True))
        attn = e * (1.0 / jnp.sum(e, axis=0, keepdims=True))
        attn2 = on_diagonal(attn)
        mixed.append(dot(v2, attn2, precision=EXACT))
        g_v = dot(g2, attn2, 1, 1, precision=EXACT)
        g_attn = jnp.where(
            half, dot(v_n[low], g2, precision=EXACT), dot(v_n[high], g2, precision=EXACT)
        )
        g_scores = attn * (g_attn - jnp.sum(g_attn * attn, axis=0, keepdims=True)) * scale
        g_scores2 = on_diagonal(g_scores)
        g_q = dot(k2, g_scores2, precision=EXACT)
        g_k = dot(q2, g_scores2, 1, 1, precision=EXACT)
        grads.append(jnp.concatenate([g_q, g_k, g_v]))
    mixed = jnp.concatenate(mixed, axis=1)
    grads = jnp.concatenate(grads, axis=1)
    g_tok = dot(jnp.concatenate(maps, axis=1), grads, precision=EXACT)
    g_num = g_tok * inverse
    g_den = jnp.where(
        den > 1.0, -jnp.sum(g_tok * tokens, axis=0, keepdims=True) * inverse, 0.0
    )

    mixed_half, num_half = mixed.astype(BF16), g_num.astype(BF16)
    table = jnp.concatenate([mixed_half, num_half])
    first = g_den.astype(BF16).astype(F32)
    second = (g_den - first).astype(BF16).astype(F32)
    third = g_den - first - second
    lines = jnp.concatenate(
        [
            table.astype(F32),
            first,
            second,
            third,
            jnp.zeros((2 * HEAD - 3, HEADS * SLICES), F32),
        ]
    )
    lines_t = lines.T.astype(BF16)
    ones = jnp.ones((2 * HEAD, points), BF16)
    row = lax.broadcasted_iota(jnp.int32, (HEAD, SLICES), 0)
    g_slice = jnp.zeros((HEAD, SLICES), F32)
    g_temp = jnp.zeros((HEAD, SLICES), F32)
    zero = jnp.zeros((), BF16)
    for pair in range(PAIRS):
        cols = slice(pair * 2 * SLICES, (pair + 1) * 2 * SLICES)
        w2 = wgt[pl.ds(pair * 2 * SLICES, 2 * SLICES), :]
        t2 = table[:, cols]
        back = dot(jnp.concatenate([jnp.where(half, t2, zero), jnp.where(half, zero, t2)]), w2)
        for i, h in enumerate((2 * pair, 2 * pair + 1)):
            rows = pl.ds(h * HEAD, HEAD)
            mrg[rows, :] = back[2 * HEAD * i : 2 * HEAD * i + HEAD].astype(BF16)
            xm = xmt[rows, :]
            right = jnp.concatenate([got[rows, :], xm, ones])
            g_w = dot(lines_t[h * SLICES : (h + 1) * SLICES], right)
            p = prob[pl.ds(h * SLICES, SLICES), :]
            g_logit = (p * live) * (g_w - jnp.sum(g_w * p, axis=0, keepdims=True))
            g_raw = (g_logit * rates[h]).astype(BF16)
            share = jnp.sum(
                jnp.sum(g_logit * logit[pl.ds(h * SLICES, SLICES), :], axis=0, keepdims=True)
                * rates[h],
                axis=1,
                keepdims=True,
            )
            g_temp = jnp.where(row == h, -share, g_temp)
            g_slice = g_slice + dot(xm, g_raw, 1, 1)
            total = back[2 * HEAD * i + HEAD : 2 * HEAD * (i + 1)] + dot(cluster, g_raw)
            gxm[rows, :] = total.astype(BF16)
    s_out[...] = jnp.concatenate([g_slice, g_temp], axis=1).reshape(PLANE, 1, 2 * SLICES)
    for i, grad in enumerate((dot(xt[...], gxm[...], 1, 1), dot(mrg[...], y_ref[...]))):
        grad = grad.astype(BF16)
        g_out[0, :, i] = grad[:, :128].reshape(16, 16, 128)
        g_out[1, :, i] = grad[:, 128:].reshape(16, 16, 128)

    def block_of(device):
        side = device // GRP
        return side // 4, lax.rem(device, GRP) * 4 + lax.rem(side, 4)

    def scatter_grads(r, carry):
        other, peer = plane_peer(r)
        col, block = block_of(other)
        push(g_out.at[col, block], g_in.at[r], 6, peer)
        push(s_out.at[other], s_in.at[r], 7, peer)
        return carry

    lax.fori_loop(1, PLANE, scatter_grads, 0)
    col, block = block_of(me)
    g_in[0] = g_out[col, block]
    s_in[0] = s_out[me]
    dx_ref[...] = dot(gxm[...], w_ref[...], 0, 1).astype(BF16)
    token_grads = dot(tokens, grads, 1, 1, precision=EXACT)
    for i in range(3):
        da_ref[i] = token_grads[:, i * HEAD : (i + 1) * HEAD]
    landed(g_in.at[pl.ds(1, PLANE - 1)], 6)
    landed(s_in.at[pl.ds(1, PLANE - 1)], 7)
    g_part[...] = jnp.sum(g_in[...].astype(F32), axis=0).astype(BF16)
    s_part[...] = jnp.sum(s_in[...], axis=0)

    def swap_grads(r, carry):
        push(g_part, g_z.at[z], 8, depth_peer(r))
        push(s_part, s_z.at[z], 9, depth_peer(r))
        return carry

    lax.fori_loop(1, depth, swap_grads, 0)
    g_z[z] = g_part[...]
    s_z[z] = s_part[...]
    landed(g_z.at[pl.ds(0, depth - 1)], 8)
    landed(s_z.at[pl.ds(0, depth - 1)], 9)
    g_sum[...] = jnp.sum(g_z[...].astype(F32), axis=0)
    s_sum[...] = jnp.sum(s_z[...], axis=0)

    def spread_grads(r, carry):
        push(g_sum, g_all.at[s], 10, side_peer(r))
        return carry

    def spread_small(r, carry):
        push(s_sum, s_all.at[me], 11, plane_peer(r)[1])
        return carry

    lax.fori_loop(1, SIDE, spread_grads, 0)
    lax.fori_loop(1, PLANE, spread_small, 0)
    g_all[s] = g_sum[...]
    s_all[me] = s_sum[...]
    landed(g_all.at[pl.ds(1, SIDE - 1)], 10)
    landed(s_all.at[pl.ds(1, PLANE - 1)], 11)
    for i in range(2):
        for side in range(SIDE):
            dw_ref[i, pl.ds(16 * (side % 4), 16), pl.ds(128 * (side // 4), 128)] = g_all[side, i]
    small = s_all[...].reshape(PLANE, 2 * SLICES)
    ds_ref[...] = small[:, :SLICES]
    at = lax.broadcasted_iota(jnp.int32, (HEADS, SLICES), 0)
    lane = lax.broadcasted_iota(jnp.int32, (HEADS, SLICES), 1)
    dt_ref[...] = jnp.sum(
        jnp.where(at == lane, small[:HEADS, SLICES:], 0.0), axis=0, keepdims=True
    )[:, :HEADS]

    left(tok_in.at[pl.ds(1, PLANE - 1)], 0)
    left(den_in.at[pl.ds(1, PLANE - 1)], 1)
    left(tok_z.at[pl.ds(0, depth - 1)], 2)
    left(den_z.at[pl.ds(0, depth - 1)], 3)
    left(tok_all.at[pl.ds(1, PLANE - 1)], 4)
    left(den_all.at[pl.ds(1, PLANE - 1)], 5)
    left(g_in.at[pl.ds(1, PLANE - 1)], 6)
    left(s_in.at[pl.ds(1, PLANE - 1)], 7)
    left(g_z.at[pl.ds(0, depth - 1)], 8)
    left(s_z.at[pl.ds(0, depth - 1)], 9)
    left(g_all.at[pl.ds(1, SIDE - 1)], 10)
    left(s_all.at[pl.ds(1, PLANE - 1)], 11)


def local(depth, x, y, w, e, c, t, a, tally):
    points, width = x.shape
    flat = HEADS * SLICES
    vmem = pl.BlockSpec(memory_space=pltpu.VMEM)
    smem = pl.BlockSpec(memory_space=pltpu.SMEM)
    lanes = 2 * SLICES
    dx, dw, ds, dt, da = pl.pallas_call(
        functools.partial(kernel, depth),
        name="layer",
        out_shape=(
            jax.ShapeDtypeStruct((points, width), BF16),
            jax.ShapeDtypeStruct((2, width // GRP, width), F32),
            jax.ShapeDtypeStruct((HEAD, SLICES), F32),
            jax.ShapeDtypeStruct((1, HEADS), F32),
            jax.ShapeDtypeStruct((3, HEAD, HEAD), F32),
        ),
        in_specs=[vmem, vmem, vmem, vmem, vmem, smem, vmem, smem],
        out_specs=[vmem] * 5,
        scratch_shapes=[
            pltpu.VMEM((width, points), BF16),
            pltpu.VMEM((width, points), BF16),
            pltpu.VMEM((flat, points), F32),
            pltpu.VMEM((flat, points), F32),
            pltpu.VMEM((flat, points), BF16),
            pltpu.VMEM((width, points), BF16),
            pltpu.VMEM((width, points), BF16),
            pltpu.VMEM((width, points), BF16),
            pltpu.VMEM((PLANE, 8, lanes), F32),
            pltpu.VMEM((PLANE, 1, lanes), F32),
            pltpu.VMEM((PLANE, 8, lanes), F32),
            pltpu.VMEM((PLANE, 1, lanes), F32),
            pltpu.VMEM((8, lanes), F32),
            pltpu.VMEM((1, lanes), F32),
            pltpu.VMEM((depth, 8, lanes), F32),
            pltpu.VMEM((depth, 1, lanes), F32),
            pltpu.VMEM((8, lanes), F32),
            pltpu.VMEM((1, lanes), F32),
            pltpu.VMEM((PLANE, 8, lanes), F32),
            pltpu.VMEM((PLANE, 1, lanes), F32),
            pltpu.VMEM((2, 16, 2, 16, 128), BF16),
            pltpu.VMEM((PLANE, 2, 16, 128), BF16),
            pltpu.VMEM((PLANE, 1, lanes), F32),
            pltpu.VMEM((PLANE, 1, lanes), F32),
            pltpu.VMEM((2, 16, 128), BF16),
            pltpu.VMEM((1, lanes), F32),
            pltpu.VMEM((depth, 2, 16, 128), BF16),
            pltpu.VMEM((depth, 1, lanes), F32),
            pltpu.VMEM((2, 16, 128), F32),
            pltpu.VMEM((1, lanes), F32),
            pltpu.VMEM((SIDE, 2, 16, 128), F32),
            pltpu.VMEM((PLANE, 1, lanes), F32),
            pltpu.SemaphoreType.DMA((12,)),
            pltpu.SemaphoreType.DMA((12,)),
        ],
        compiler_params=pltpu.CompilerParams(
            collective_id=0, has_side_effects=True, vmem_limit_bytes=40 * 1024 * 1024
        ),
    )(x, y, w, e, c, t, a, tally)
    return dx, dw, ds, dt.reshape(HEADS), da


def solution(mesh):
    depth = mesh.devices.size // PLANE
    finer = Mesh(mesh.devices.reshape(depth, SIDE, GRP), ("z", "s", "y"))
    rows = P(("z", "s", "y"), None)
    return jax.shard_map(
        functools.partial(local, depth),
        mesh=finer,
        in_specs=(rows, rows, P(), P(), P(), P(), P(), P()),
        out_specs=(rows, P(None, "y", None), P(), P(), P()),
        check_vma=False,
    )
```

time: 220 us -> 79.3 us (0.36); the launches traced: 217 us -> 79 us
  waiting for transfers between devices: 72 us -> 0 us
  blocking collectives: 71.6 us -> 0 us
  Pallas kernels: 0 us -> 68.7 us
  starting transfers between devices: 29 us -> 0 us
  matrix products: 13.5 us -> 0 us
  local copies, waits for them, and re-layouts: 22.1 us -> 9.63 us
  other arithmetic: 7.73 us -> 0 us
    all_to_all x6 -> x0, waiting for transfers between devices: 72 us -> none  [the longest x4 52.1 us: from_everyone(): return lax.all_to_all(copies, axis, split_axis=0, concat_axis=0, tiled=True)]
    all_to_all x5 -> x0, blocking collectives: 71.6 us -> none  [the longest x1 28.1 us: sum_by_axis(): lax.all_to_all(nearer, far, split_axis=0, concat_axis=0, tiled=True)]
    pallas_call x0 -> x1, Pallas kernels: none -> 68.7 us  [local(): pl.pallas_call(functools.partial(kernel, depth), name='layer', out_shape=...]
    all_to_all x6 -> x0, starting transfers between devices: 29 us -> none  [the longest x4 21 us: from_everyone(): return lax.all_to_all(copies, axis, split_axis=0, concat_axis=0, tiled=True)]
    dot_general x28 -> x0, matrix products: 13.1 us -> none  [the longest x1 1.33 us: segment_forward_sweep(): jnp.dot(xm, slice_wide_weights, preferred_element_type=jnp.float32)]
    mul x6 -> x0, local copies, waits for them, and re-layouts: 4.41 us -> none  [block_diagonal(): spread_out = unit_matrix[:, None, :, None] * parts[:, :, None, :]]
    broadcast_in_dim x6 -> x0, local copies, waits for them, and re-layouts: 3.16 us -> none  [from_everyone(): copies = jnp.broadcast_to(shard, (lax.axis_size(axis), *shard.shape))]
    unnamed x59 -> x21, local copies, waits for them, and re-layouts: 8.1 us -> 9.63 us
  transfers between devices with their start and end apart: 6 -> 0, of which waited for: 6 -> 0; matrix products, arithmetic and copies ran while one was open for 2% -> 0% of each run, Pallas kernels for 0% -> 0%
where the time goes in v1:
time: 79.3 us; the launch traced here: 79 us
  Pallas kernels  68.7 us (87%)
  local copies, waits for them, and re-layouts  9.63 us (12%)
    pallas_call x1, Pallas kernels, local(): pl.pallas_call(functools.partial(kernel, depth), name='layer', out_shape=...  68.7 us
    unnamed x21, local copies, waits for them, and re-layouts  9.63 us

profile of v1, /device:TPU:1, one launch (start us, length us, event | category | flops | bytes accessed | tf_op | source)
XLA Modules:
  0.0 79.0 jit_solution(7295936899128091367)
XLA Ops:
  0.6 0.0 copy-start
  0.6 0.9 %copy-done = bf16[512,256]{1,0:T(8,128)(2,1)S(1)} copy-done((bf16[512,256]{1,0:T(8,128)(2,1)S(1)}, bf16[512,256]{1,0:T(8,128)(2,1)}, u32[]{:S(2)}) %copy-start) | copy-done | bytes 262168
  1.6 0.0 copy-start.1
  1.6 0.9 %copy-done.1 = bf16[512,256]{1,0:T(8,128)(2,1)S(1)} copy-done((bf16[512,256]{1,0:T(8,128)(2,1)S(1)}, bf16[512,256]{1,0:T(8,128)(2,1)}, u32[]{:S(2)}) %copy-start.1) | copy-done | bytes 262168
  2.5 0.0 copy-start.2
  2.5 0.9 %copy-done.2 = bf16[256,256]{1,0:T(8,128)(2,1)S(1)} copy-done((bf16[256,256]{1,0:T(8,128)(2,1)S(1)}, bf16[256,256]{1,0:T(8,128)(2,1)}, u32[]{:S(2)}) %copy-start.2) | copy-done | bytes 131096
  3.4 0.0 copy-start.3
  3.4 0.9 %copy-done.3 = bf16[256,256]{1,0:T(8,128)(2,1)S(1)} copy-done((bf16[256,256]{1,0:T(8,128)(2,1)S(1)}, bf16[256,256]{1,0:T(8,128)(2,1)}, u32[]{:S(2)}) %copy-start.3) | copy-done | bytes 131096
  4.3 0.0 copy-start.4
  4.3 0.8 %copy-done.4 = f32[3,32,32]{2,1,0:T(8,128)S(1)} copy-done((f32[3,32,32]{2,1,0:T(8,128)S(1)}, f32[3,32,32]{2,1,0:T(8,128)}, u32[]{:S(2)}) %copy-start.4) | copy-done | bytes 12312
  5.1 0.0 copy-start.5
  5.1 0.7 copy-done.5
  5.8 0.0 copy-start.6
  5.8 0.7 copy-done.6
  6.5 0.0 copy-start.7
  6.5 0.7 copy-done.7
  7.2 68.7 %layer.1 = (bf16[512,256]{1,0:T(8,128)(2,1)S(1)}, f32[2,64,256]{2,1,0:T(8,128)S(1)}, f32[32,64]{1,0:T(8,128)S(1)}, f32[1,8]{1,0:T(1,128)S(1)}, f32[3,32,32]{2,1,0:T(8,128)S(1)}) custom-call(bf16[512,256]{1,0:T(8,128)(2,1)S(1)} %copy-done, bf16[512,256]{1,0:T(8,128)(2,1)S(1)} %copy-done.1, bf16[256,256]{1,0:T(8,128)(2,1)S(1)} %copy-done.2, ...), custom_call_target="tpu_custom_call" | custom-call | tf_op jit(solution)/shard_map/layer/pallas_call | solution.py:376
  75.9 0.7 copy.18
  76.6 0.7 copy.19
  77.2 0.6 copy.20
  77.9 0.5 copy.21
  78.4 0.6 copy.22
Async XLA Ops:
  0.6 1.0 %copy-start = (bf16[512,256]{1,0:T(8,128)(2,1)S(1)}, bf16[512,256]{1,0:T(8,128)(2,1)}, u32[]{:S(2)}) copy-start(bf16[512,256]{1,0:T(8,128)(2,1)} %x_ref.1) | copy-start | bytes 786436
  1.6 0.9 %copy-start.1 = (bf16[512,256]{1,0:T(8,128)(2,1)S(1)}, bf16[512,256]{1,0:T(8,128)(2,1)}, u32[]{:S(2)}) copy-start(bf16[512,256]{1,0:T(8,128)(2,1)} %y_ref.1) | copy-start | bytes 786436
  2.5 0.9 %copy-start.2 = (bf16[256,256]{1,0:T(8,128)(2,1)S(1)}, bf16[256,256]{1,0:T(8,128)(2,1)}, u32[]{:S(2)}) copy-start(bf16[256,256]{1,0:T(8,128)(2,1)} %w_ref.1) | copy-start | bytes 393220
  3.4 0.9 %copy-start.3 = (bf16[256,256]{1,0:T(8,128)(2,1)S(1)}, bf16[256,256]{1,0:T(8,128)(2,1)}, u32[]{:S(2)}) copy-start(bf16[256,256]{1,0:T(8,128)(2,1)} %e_ref.1) | copy-start | bytes 393220
  4.3 0.8 %copy-start.4 = (f32[3,32,32]{2,1,0:T(8,128)S(1)}, f32[3,32,32]{2,1,0:T(8,128)}, u32[]{:S(2)}) copy-start(f32[3,32,32]{2,1,0:T(8,128)} %a_ref.1) | copy-start | bytes 36868
  5.1 0.7 copy-start.5
  5.8 0.7 copy-start.6
  6.5 0.7 copy-start.7
